TPU v7x, 512 devices: a whole 4x4x16 slice. The times are simulated.
512 devices in a mesh: dp: 8 (over z_lo), row: 16 (over z_hi, x, core), col: 4 (over y).
Axes of the slice: x: 4, y: 4, z: 16 (z_hi: 2, z_lo: 8; z = z_hi * 8 + z_lo), core: 2. Of those that a mesh axis runs over, the one named last changes fastest.
Arguments:
- expand_gradient: bfloat16 [8, 4096, 5120], P('dp', 'row', 'col'), may hold values from -24 to 24, as said below
- expand_master: float32 [4096, 5120], P(('row', 'dp'), 'col'), may hold values from -0.12 to 0.12
- expand_rows: float32 [4096], P(('row', 'dp')), may hold values from 0.01 to 1
- expand_columns: float32 [5120], P('col'), may hold values from 0.01 to 1
- contract_gradient: bfloat16 [8, 5120, 4096], P('dp', 'row', 'col'), may hold values from -24 to 24, as said below
- contract_master: float32 [5120, 4096], P(('row', 'dp'), 'col'), may hold values from -0.12 to 0.12
- contract_rows: float32 [5120], P(('row', 'dp')), may hold values from 0.01 to 1
- contract_columns: float32 [4096], P('col'), may hold values from 0.01 to 1
- attend_gradient: bfloat16 [8, 4096, 4096], P('dp', 'row', 'col'), may hold values from -24 to 24, as said below
- attend_master: float32 [4096, 4096], P(('row', 'dp'), 'col'), may hold values from -0.12 to 0.12
- attend_rows: float32 [4096], P(('row', 'dp')), may hold values from 0.01 to 1
- attend_columns: float32 [4096], P('col'), may hold values from 0.01 to 1
Outputs:
- expand_updated: float32 [4096, 5120], P(('row', 'dp'), 'col')
- expand_weights: bfloat16 [4096, 5120], P('row', 'col')
- expand_rows_next: float32 [4096], P(('row', 'dp'))
- expand_columns_next: float32 [5120], P('col')
- expand_step: float32 [4096, 5120], P(('row', 'dp'), 'col')
- contract_updated: float32 [5120, 4096], P(('row', 'dp'), 'col')
- contract_weights: bfloat16 [5120, 4096], P('row', 'col')
- contract_rows_next: float32 [5120], P(('row', 'dp'))
- contract_columns_next: float32 [4096], P('col')
- contract_step: float32 [5120, 4096], P(('row', 'dp'), 'col')
- attend_updated: float32 [4096, 4096], P(('row', 'dp'), 'col')
- attend_weights: bfloat16 [4096, 4096], P('row', 'col')
- attend_rows_next: float32 [4096], P(('row', 'dp'))
- attend_columns_next: float32 [4096], P('col')
- attend_step: float32 [4096, 4096], P(('row', 'dp'), 'col')
Inputs may be any that keep to these rules, and one draw needn't show every extreme that they name: `expand_gradient`: each replica's gradient, of any scale from entry to entry. `contract_gradient`: each replica's gradient, of any scale from entry to entry. `attend_gradient`: each replica's gradient, of any scale from entry to entry.
All inputs are finite; a program needn't handle non-finite values.
Results may differ from a plain program's by a relative error of at most 0.0004.
Values may be sent and summed in bfloat16 or wider, within the bound.
A program may use at most 64 MiB of HBM per device.

v0:
```python
import jax
import jax.numpy as jnp
from jax import lax
from jax.sharding import Mesh
from jax.sharding import PartitionSpec as P

ROW = ("row_0", "row_1", "row_2")
DP_ROW = ("dp", "row_0", "row_1", "row_2")
DP_ROW_COL = ("dp", "row_0", "row_1", "row_2", "col")
ROW_DP = ("row_0", "row_1", "row_2", "dp")
tiny_square = 1e-30
decay_rate = 0.9
learn_rate = 0.01


def in_order(blocks, dim):
    blocks = jnp.moveaxis(blocks, 0, dim)
    lengths = blocks.shape
    return blocks.reshape(*lengths[:dim], lengths[dim] * lengths[dim + 1], *lengths[dim + 2 :])


def from_everyone(shard, axis):
    copies = jnp.broadcast_to(shard, (lax.axis_size(axis), *shard.shape))
    return lax.all_to_all(copies, axis, split_axis=0, concat_axis=0, tiled=True)


def collect(shard, axis, dim):
    return in_order(from_everyone(shard, axis), dim)


def taken_together(shard, axis):
    everything = from_everyone(shard, axis)
    return jnp.sum(everything, axis=0)


def packed_total(arrays, axis):
    ends = [0]
    for a in arrays:
        ends.append(ends[-1] + a.size)
    subtotal = taken_together(jnp.concatenate([a.ravel() for a in arrays]), axis)
    return tuple((subtotal[b:e].reshape(a.shape) for a, b, e in zip(arrays, ends, ends[1:])))


def one_axis_at_a_time(shard, axes):
    for axis in axes:
        shard = lax.psum(shard, axis)
    return shard


def finish(update_raw, clip_total, master, full_size):
    clip_scale = jnp.maximum(1.0, jnp.sqrt(clip_total / full_size))
    step_taken = update_raw / clip_scale
    updated = master - learn_rate * step_taken
    weights = collect(updated.astype(jnp.bfloat16), "dp", 0)
    return (updated, weights, step_taken)


def reduce_gradient(gradient, dp_count):
    received = lax.all_to_all(gradient, "dp", split_axis=1, concat_axis=0, tiled=True)
    summed = jnp.sum(received.astype(jnp.float32), axis=0)
    return summed / dp_count


def body(
    expand_gradient,
    expand_master,
    expand_rows,
    expand_columns,
    contract_gradient,
    contract_master,
    contract_rows,
    contract_columns,
    attend_gradient,
    attend_master,
    attend_rows,
    attend_columns,
):
    groups = (
        (expand_gradient, expand_master, expand_rows, expand_columns),
        (contract_gradient, contract_master, contract_rows, contract_columns),
        (attend_gradient, attend_master, attend_rows, attend_columns),
    )
    dp_count = lax.axis_size("dp")
    col_count = lax.axis_size("col")
    split_count = dp_count * lax.axis_size(ROW)
    means = []
    for gradient, master, row_stat, column_stat in groups:
        means.append(reduce_gradient(gradient, dp_count))
    squares = [mean_grad * mean_grad + tiny_square for mean_grad in means]
    row_parts = [jnp.sum(square_block, axis=1) for square_block in squares]
    column_parts = [jnp.sum(square_block, axis=0) for square_block in squares]
    heights = [mean_grad.shape[0] * split_count for mean_grad in means]
    widths = [mean_grad.shape[1] * col_count for mean_grad in means]
    outputs = []
    row_totals = packed_total((row_parts[0], row_parts[1], row_parts[2]), "col")
    rows_next = [
        decay_rate * groups[which][2] + (1.0 - decay_rate) * row_totals[which] / widths[which]
        for which in range(3)
    ]
    joined = (
        one_axis_at_a_time(column_parts[0], DP_ROW),
        one_axis_at_a_time(column_parts[1], DP_ROW),
        one_axis_at_a_time(column_parts[2], DP_ROW),
        one_axis_at_a_time(jnp.sum(rows_next[0]), DP_ROW),
        one_axis_at_a_time(jnp.sum(rows_next[1]), DP_ROW),
        one_axis_at_a_time(jnp.sum(rows_next[2]), DP_ROW),
    )
    columns_next = [
        decay_rate * groups[which][3] + (1.0 - decay_rate) * joined[which] / heights[which]
        for which in range(3)
    ]
    raws = [
        means[which]
        * jnp.sqrt(
            joined[3 + which]
            / heights[which]
            / (rows_next[which][:, None] * columns_next[which][None, :])
        )
        for which in range(3)
    ]
    clips = (
        one_axis_at_a_time(jnp.sum(raws[0] * raws[0]), DP_ROW_COL),
        one_axis_at_a_time(jnp.sum(raws[1] * raws[1]), DP_ROW_COL),
        one_axis_at_a_time(jnp.sum(raws[2] * raws[2]), DP_ROW_COL),
    )
    for which in range(3):
        updated, weights, step_taken = finish(
            raws[which], clips[which], groups[which][1], heights[which] * widths[which]
        )
        outputs.extend([updated, weights, rows_next[which], columns_next[which], step_taken])
    return tuple(outputs)


def solution(mesh):
    finer = Mesh(
        mesh.devices.reshape(mesh.shape["dp"], 2, 4, 2, mesh.shape["col"]),
        ("dp", "row_0", "row_1", "row_2", "col"),
    )
    in_specs = (
        P("dp", ROW, "col"),
        P(ROW_DP, "col"),
        P(ROW_DP),
        P("col"),
        P("dp", ROW, "col"),
        P(ROW_DP, "col"),
        P(ROW_DP),
        P("col"),
        P("dp", ROW, "col"),
        P(ROW_DP, "col"),
        P(ROW_DP),
        P("col"),
    )
    out_specs = (
        P(ROW_DP, "col"),
        P(ROW, "col"),
        P(ROW_DP),
        P("col"),
        P(ROW_DP, "col"),
        P(ROW_DP, "col"),
        P(ROW, "col"),
        P(ROW_DP),
        P("col"),
        P(ROW_DP, "col"),
        P(ROW_DP, "col"),
        P(ROW, "col"),
        P(ROW_DP),
        P("col"),
        P(ROW_DP, "col"),
    )
    return jax.shard_map(body, mesh=finer, in_specs=in_specs, out_specs=out_specs, check_vma=False)
```

profile of v0, /device:TPU:2, one launch (start us, length us, event | category | flops | bytes accessed | tf_op | source)
XLA Modules:
  0.0 415.7 jit_solution(8251407359261963405)
XLA Ops:
  0.6 1.9 copy.54
  2.5 0.5 broadcast.40
  3.0 3.7 reduce.2
  6.7 1.2 reshape.72
  7.9 12.5 %all-to-all-start.2 = ((bf16[8,2,16384]{2,1,0:T(2,128)(2,1)}), bf16[8,2,16384]{2,1,0:T(2,128)(2,1)S(1)}, u32[]{:S(2)}, u32[]{:S(2)}) async-start(bf16[8,2,16384]{2,1,0:T(2,128)(2,1)} %reshape.72), calls=%async_computation.2 | async-start | bytes 1048576 | tf_op jit(solution)/shard_map/all_to_all | solution.py:59
  20.4 1.0 copy.53
  21.4 4.6 %reduce.1 = bf16[256,1280]{1,0:T(8,128)(2,1)S(1)} reduce(bf16[256,1,1280]{2,1,0:T(2,128)(2,1)S(1)} %bitcast.23, bf16[]{:T(256)} %broadcast.40), dimensions={1}, to_apply=%bitcast.20.reduce_sub_computation | reduce | bytes 1310722
  26.1 0.0 copy-start.3
  26.1 1.0 reshape.70
  27.1 22.1 %all-to-all-done.2 = bf16[8,2,16384]{2,1,0:T(2,128)(2,1)S(1)} async-done(((bf16[8,2,16384]{2,1,0:T(2,128)(2,1)}), bf16[8,2,16384]{2,1,0:T(2,128)(2,1)S(1)}, u32[]{:S(2)}, u32[]{:S(2)}) %all-to-all-start.2) | async-done | bytes 524320 | tf_op jit(solution)/shard_map/all_to_all | solution.py:59
  49.2 0.8 copy-done
  49.9 4.3 %all-to-all-start = ((bf16[8,2,20480]{2,1,0:T(2,128)(2,1)}), bf16[8,2,20480]{2,1,0:T(2,128)(2,1)S(1)}, u32[]{:S(2)}, u32[]{:S(2)}) async-start(bf16[8,2,20480]{2,1,0:T(2,128)(2,1)} %reshape.70), calls=%async_computation | async-start | bytes 1310720 | tf_op jit(solution)/shard_map/all_to_all | solution.py:59
  54.2 1.0 copy.52
  55.2 4.5 %reduce.3 = bf16[320,1024]{1,0:T(8,128)(2,1)S(1)} reduce(bf16[320,1,1024]{2,1,0:T(2,128)(2,1)S(1)} %bitcast.22, bf16[]{:T(256)} %broadcast.40), dimensions={1}, to_apply=%bitcast.19.reduce_sub_computation | reduce | bytes 1310722
  59.7 1.3 reshape.74
  61.0 27.3 %all-to-all-done = bf16[8,2,20480]{2,1,0:T(2,128)(2,1)S(1)} async-done(((bf16[8,2,20480]{2,1,0:T(2,128)(2,1)}), bf16[8,2,20480]{2,1,0:T(2,128)(2,1)S(1)}, u32[]{:S(2)}, u32[]{:S(2)}) %all-to-all-start) | async-done | bytes 655392 | tf_op jit(solution)/shard_map/all_to_all | solution.py:59
  88.2 4.3 %all-to-all-start.1 = ((bf16[8,2,20480]{2,1,0:T(2,128)(2,1)}), bf16[8,2,20480]{2,1,0:T(2,128)(2,1)S(1)}, u32[]{:S(2)}, u32[]{:S(2)}) async-start(bf16[8,2,20480]{2,1,0:T(2,128)(2,1)} %reshape.74), calls=%async_computation.1 | async-start | bytes 1310720 | tf_op jit(solution)/shard_map/all_to_all | solution.py:59
  92.5 0.5 reshape.73
  93.1 0.2 copy.47
  93.2 0.1 convert_reduce_fusion.2
  93.3 0.1 fusion.4
  93.5 0.7 reshape.71
  94.1 0.1 copy.43
  94.2 0.1 convert_reduce_fusion.1
  94.3 0.1 fusion.1
  94.4 31.9 %all-to-all-done.1 = bf16[8,2,20480]{2,1,0:T(2,128)(2,1)S(1)} async-done(((bf16[8,2,20480]{2,1,0:T(2,128)(2,1)}), bf16[8,2,20480]{2,1,0:T(2,128)(2,1)S(1)}, u32[]{:S(2)}, u32[]{:S(2)}) %all-to-all-start.1) | async-done | bytes 655392 | tf_op jit(solution)/shard_map/all_to_all | solution.py:59
  126.4 0.6 reshape.75
  127.0 0.0 copy-start.16
  127.0 0.0 copy-start.17
  127.1 0.0 copy-start.14
  127.1 0.2 copy.45
  127.3 0.1 convert_reduce_fusion
  127.4 0.1 fusion.2
  127.6 0.1 pad_maximum_fusion
  127.7 9.5 %all_to_all.48 = f32[4,1,104]{2,1,0:T(1,128)S(1)} all-to-all(f32[4,1,104]{2,1,0:T(1,128)S(1)} %broadcast_in_dim.8), channel_id=1, replica_groups=mesh['dp'=8,'row_0'=2,'row_1'=4,'row_2'=2,'col'=4] {'col'}, dimensions={0} | all-to-all | bytes 3328 | tf_op jit(solution)/shard_map/all_to_all | solution.py:24
  137.2 0.7 fusion.10
  137.9 0.7 fusion.9
  138.6 52.8 %all-reduce.1 = (f32[1280]{0:T(1024)S(1)}, f32[]{:T(128)}, f32[1024]{0:T(1024)S(1)}, f32[]{:T(128)}, f32[1024]{0:T(1024)S(1)}, /*index=5*/f32[]{:T(128)}) all-reduce(f32[1280]{0:T(1024)S(1)} %get-tuple-element.18, f32[]{:T(128)} %get-tuple-element.75, ...), channel_id=1, replica_groups=mesh['dp'=8,'row_0'=2,'row_1'=4,'row_2'=2,'col'=4] {'dp'}, use_global_device_ids=true, to_apply=%region_13.0 | all-reduce | flops 3331 | bytes 26648 | tf_op jit(solution)/shard_map/psum | solution.py:46
  191.4 23.0 %all-reduce.8 = (f32[1280]{0:T(1024)S(1)}, f32[]{:T(128)}, f32[1024]{0:T(1024)S(1)}, f32[]{:T(128)}, f32[1024]{0:T(1024)S(1)}, /*index=5*/f32[]{:T(128)}) all-reduce(f32[1280]{0:T(1024)S(1)} %get-tuple-element.24, f32[]{:T(128)} %get-tuple-element.25, ...), channel_id=1, replica_groups=mesh['dp'=8,'row_0'=2,'row_1'=4,'row_2'=2,'col'=4] {'row_0'}, use_global_device_ids=true, to_apply=%region_14.0 | all-reduce | flops 3331 | bytes 26648 | tf_op jit(solution)/shard_map/psum | solution.py:46
  214.4 15.2 %all-reduce.4 = (f32[1280]{0:T(1024)S(1)}, f32[]{:T(128)}, f32[1024]{0:T(1024)S(1)}, f32[]{:T(128)}, f32[1024]{0:T(1024)S(1)}, /*index=5*/f32[]{:T(128)}) all-reduce(f32[1280]{0:T(1024)S(1)} %get-tuple-element.54, f32[]{:T(128)} %get-tuple-element.55, ...), channel_id=1, replica_groups=mesh['dp'=8,'row_0'=2,'row_1'=4,'row_2'=2,'col'=4] {'row_1'}, use_global_device_ids=true, to_apply=%region_15.0 | all-reduce | flops 3331 | bytes 26648 | tf_op jit(solution)/shard_map/psum | solution.py:46
  229.6 4.5 %all-reduce.6 = (f32[1280]{0:T(1024)S(1)}, f32[]{:T(128)}, f32[1024]{0:T(1024)S(1)}, f32[]{:T(128)}, f32[1024]{0:T(1024)S(1)}, /*index=5*/f32[]{:T(128)}) all-reduce(f32[1280]{0:T(1024)S(1)} %get-tuple-element.36, f32[]{:T(128)} %get-tuple-element.37, ...), channel_id=1, replica_groups=mesh['dp'=8,'row_0'=2,'row_1'=4,'row_2'=2,'col'=4] {'row_2'}, use_global_device_ids=true, to_apply=%region_16.0 | all-reduce | flops 3331 | bytes 26648 | tf_op jit(solution)/shard_map/psum | solution.py:46
  236.0 0.8 multiply_reduce_fusion.1
  236.8 0.8 multiply_reduce_fusion
  237.6 0.7 multiply_reduce_fusion.2
  238.3 25.7 %all-reduce = (f32[]{:T(128)}, f32[]{:T(128)}, f32[]{:T(128)}) all-reduce(f32[]{:T(128)} %multiply_reduce_fusion.1, f32[]{:T(128)} %multiply_reduce_fusion, f32[]{:T(128)} %multiply_reduce_fusion.2), channel_id=1, replica_groups=mesh['dp'=8,'row_0'=2,'row_1'=4,'row_2'=2,'col'=4] {'dp'}, use_global_device_ids=true, to_apply=%region_18.0 | all-reduce | flops 3 | bytes 24 | tf_op jit(solution)/shard_map/psum | solution.py:46
  264.0 14.3 %all-reduce.7 = (f32[]{:T(128)}, f32[]{:T(128)}, f32[]{:T(128)}) all-reduce(f32[]{:T(128)} %get-tuple-element.21, f32[]{:T(128)} %get-tuple-element.22, f32[]{:T(128)} %get-tuple-element.23), channel_id=1, replica_groups=mesh['dp'=8,'row_0'=2,'row_1'=4,'row_2'=2,'col'=4] {'row_0'}, use_global_device_ids=true, to_apply=%region_19.0 | all-reduce | flops 3 | bytes 24 | tf_op jit(solution)/shard_map/psum | solution.py:46
  278.2 11.8 %all-reduce.3 = (f32[]{:T(128)}, f32[]{:T(128)}, f32[]{:T(128)}) all-reduce(f32[]{:T(128)} %get-tuple-element.51, f32[]{:T(128)} %get-tuple-element.52, f32[]{:T(128)} %get-tuple-element.53), channel_id=1, replica_groups=mesh['dp'=8,'row_0'=2,'row_1'=4,'row_2'=2,'col'=4] {'row_1'}, use_global_device_ids=true, to_apply=%region_20.0 | all-reduce | flops 3 | bytes 24 | tf_op jit(solution)/shard_map/psum | solution.py:46
  290.1 3.1 all-reduce.5
  293.2 9.5 %all-reduce.2 = (f32[]{:T(128)}, f32[]{:T(128)}, f32[]{:T(128)}) all-reduce(f32[]{:T(128)} %get-tuple-element.42, f32[]{:T(128)} %get-tuple-element.43, f32[]{:T(128)} %get-tuple-element.44), channel_id=1, replica_groups=mesh['dp'=8,'row_0'=2,'row_1'=4,'row_2'=2,'col'=4] {'col'}, use_global_device_ids=true, to_apply=%region_22.0 | all-reduce | flops 3 | bytes 24 | tf_op jit(solution)/shard_map/psum | solution.py:46
  303.4 0.8 fusion.6
  304.2 0.9 broadcast_in_dim.21
  305.1 3.5 all-to-all-start.6
  309.3 0.9 fusion.8
  310.2 25.6 %all-to-all-done.6 = bf16[8,32,1024]{2,1,0:T(8,128)(2,1)S(1)} async-done(((bf16[8,32,1024]{2,1,0:T(8,128)(2,1)}), bf16[8,32,1024]{2,1,0:T(8,128)(2,1)S(1)}, u32[]{:S(2)}, u32[]{:S(2)}) %all-to-all-start.6) | async-done | bytes 524320 | tf_op jit(solution)/shard_map/all_to_all | solution.py:24
  335.8 0.9 broadcast_in_dim.9
  336.7 4.3 %all-to-all-start.4 = ((bf16[8,32,1280]{2,1,0:T(8,128)(2,1)}), bf16[8,32,1280]{2,1,0:T(8,128)(2,1)S(1)}, u32[]{:S(2)}, u32[]{:S(2)}) async-start(bf16[8,32,1280]{2,1,0:T(8,128)(2,1)} %broadcast_in_dim.9), calls=%async_computation.4 | async-start | bytes 1310720 | tf_op jit(solution)/shard_map/all_to_all | solution.py:24
  341.7 0.9 fusion.7
  342.6 32.0 %all-to-all-done.4 = bf16[8,32,1280]{2,1,0:T(8,128)(2,1)S(1)} async-done(((bf16[8,32,1280]{2,1,0:T(8,128)(2,1)}), bf16[8,32,1280]{2,1,0:T(8,128)(2,1)S(1)}, u32[]{:S(2)}, u32[]{:S(2)}) %all-to-all-start.4) | async-done | bytes 655392 | tf_op jit(solution)/shard_map/all_to_all | solution.py:24
  374.6 0.9 broadcast_in_dim.20
  375.5 4.3 %all-to-all-start.5 = ((bf16[8,40,1024]{2,1,0:T(8,128)(2,1)}), bf16[8,40,1024]{2,1,0:T(8,128)(2,1)S(1)}, u32[]{:S(2)}, u32[]{:S(2)}) async-start(bf16[8,40,1024]{2,1,0:T(8,128)(2,1)} %broadcast_in_dim.20), calls=%async_computation.5 | async-start | bytes 1310720 | tf_op jit(solution)/shard_map/all_to_all | solution.py:24
  379.8 33.5 %all-to-all-done.5 = bf16[8,40,1024]{2,1,0:T(8,128)(2,1)S(1)} async-done(((bf16[8,40,1024]{2,1,0:T(8,128)(2,1)}), bf16[8,40,1024]{2,1,0:T(8,128)(2,1)S(1)}, u32[]{:S(2)}, u32[]{:S(2)}) %all-to-all-start.5) | async-done | bytes 655392 | tf_op jit(solution)/shard_map/all_to_all | solution.py:24
  413.3 0.8 copy.58
  414.1 0.8 copy.59
  415.0 0.8 copy.60
  (37 shorter events, 0.1 us)
Async XLA Ops:
  6.7 13.7 %copy-start.2 = (bf16[1,256,1280]{2,1,0:T(8,128)(2,1)S(1)}, bf16[1,256,1280]{2,1,0:T(8,128)(2,1)}, u32[]{:S(2)}) copy-start(bf16[1,256,1280]{2,1,0:T(8,128)(2,1)} %param.12) | copy-start | bytes 1966084
  7.9 41.3 %all-to-all-start.2 = ((bf16[8,2,16384]{2,1,0:T(2,128)(2,1)}), bf16[8,2,16384]{2,1,0:T(2,128)(2,1)S(1)}, u32[]{:S(2)}, u32[]{:S(2)}) async-start(bf16[8,2,16384]{2,1,0:T(2,128)(2,1)} %reshape.72), calls=%async_computation.2 | async-start | bytes 1048576 | tf_op jit(solution)/shard_map/all_to_all | solution.py:59
  26.1 28.1 %copy-start.3 = (bf16[1,320,1024]{2,1,0:T(8,128)(2,1)S(1)}, bf16[1,320,1024]{2,1,0:T(8,128)(2,1)}, u32[]{:S(2)}) copy-start(bf16[1,320,1024]{2,1,0:T(8,128)(2,1)} %param.16) | copy-start | bytes 1966084
  49.2 0.8 copy-start
  49.9 38.3 %all-to-all-start = ((bf16[8,2,20480]{2,1,0:T(2,128)(2,1)}), bf16[8,2,20480]{2,1,0:T(2,128)(2,1)S(1)}, u32[]{:S(2)}, u32[]{:S(2)}) async-start(bf16[8,2,20480]{2,1,0:T(2,128)(2,1)} %reshape.70), calls=%async_computation | async-start | bytes 1310720 | tf_op jit(solution)/shard_map/all_to_all | solution.py:59
  61.0 31.6 %copy-start.1 = (bf16[8,2,16384]{2,1,0:T(2,128)(2,1)S(1)}, bf16[8,2,16384]{2,1,0:T(2,128)(2,1)}, u32[]{:S(2)}) copy-start(bf16[8,2,16384]{2,1,0:T(2,128)(2,1)} %copy-done) | copy-start | bytes 1572868
  88.2 38.2 %all-to-all-start.1 = ((bf16[8,2,20480]{2,1,0:T(2,128)(2,1)}), bf16[8,2,20480]{2,1,0:T(2,128)(2,1)S(1)}, u32[]{:S(2)}, u32[]{:S(2)}) async-start(bf16[8,2,20480]{2,1,0:T(2,128)(2,1)} %reshape.74), calls=%async_computation.1 | async-start | bytes 1310720 | tf_op jit(solution)/shard_map/all_to_all | solution.py:59
  127.0 10.2 %copy-start.16 = (f32[40]{0:T(128)S(1)}, f32[40]{0:T(128)}, u32[]{:S(2)}) copy-start(f32[40]{0:T(128)} %param.18) | copy-start | bytes 484
  127.0 10.9 %copy-start.17 = (f32[32]{0:T(128)S(1)}, f32[32]{0:T(128)}, u32[]{:S(2)}) copy-start(f32[32]{0:T(128)} %param.22) | copy-start | bytes 388
  127.0 10.8 %copy-start.18 = (f32[32]{0:T(128)S(1)}, f32[32]{0:T(128)}, u32[]{:S(2)}) copy-start(f32[32]{0:T(128)} %param.14) | copy-start | bytes 388
  127.1 108.3 %copy-start.10 = (f32[1280]{0:T(1024)S(1)}, f32[1280]{0:T(1024)}, u32[]{:S(2)}) copy-start(f32[1280]{0:T(1024)} %param.15) | copy-start | bytes 15364
  127.1 109.7 %copy-start.14 = (f32[1024]{0:T(1024)S(1)}, f32[1024]{0:T(1024)}, u32[]{:S(2)}) copy-start(f32[1024]{0:T(1024)} %param.23) | copy-start | bytes 12292
  127.1 109.7 %copy-start.15 = (f32[1024]{0:T(1024)S(1)}, f32[1024]{0:T(1024)}, u32[]{:S(2)}) copy-start(f32[1024]{0:T(1024)} %param.19) | copy-start | bytes 12292
  127.3 176.0 %copy-start.6 = (f32[32,1024]{1,0:T(8,128)S(1)}, f32[32,1024]{1,0:T(8,128)}, u32[]{:S(2)}) copy-start(f32[32,1024]{1,0:T(8,128)} %param.21) | copy-start | bytes 393220
  137.9 203.8 %copy-start.11 = (f32[40]{0:T(128)}, f32[40]{0:T(128)S(1)}, u32[]{:S(2)}) copy-start(f32[40]{0:T(128)S(1)} %get-tuple-element.101) | copy-start | bytes 484
  138.6 166.5 %copy-start.13 = (f32[32]{0:T(128)}, f32[32]{0:T(128)S(1)}, u32[]{:S(2)}) copy-start(f32[32]{0:T(128)S(1)} %get-tuple-element.106) | copy-start | bytes 388
  138.6 170.7 %copy-start.12 = (f32[32]{0:T(128)}, f32[32]{0:T(128)S(1)}, u32[]{:S(2)}) copy-start(f32[32]{0:T(128)S(1)} %get-tuple-element.96) | copy-start | bytes 388
  235.4 73.9 %copy-start.7 = (f32[1280]{0:T(1024)}, f32[1280]{0:T(1024)S(1)}, u32[]{:S(2)}) copy-start(f32[1280]{0:T(1024)S(1)} %multiply_add_fusion.3) | copy-start | bytes 15364
  236.8 72.5 %copy-start.4 = (f32[32,1280]{1,0:T(8,128)S(1)}, f32[32,1280]{1,0:T(8,128)}, u32[]{:S(2)}) copy-start(f32[32,1280]{1,0:T(8,128)} %param.13) | copy-start | bytes 491524
  236.8 73.4 %copy-start.8 = (f32[1024]{0:T(1024)}, f32[1024]{0:T(1024)S(1)}, u32[]{:S(2)}) copy-start(f32[1024]{0:T(1024)S(1)} %get-tuple-element.107) | copy-start | bytes 12292
  236.8 104.9 %copy-start.9 = (f32[1024]{0:T(1024)}, f32[1024]{0:T(1024)S(1)}, u32[]{:S(2)}) copy-start(f32[1024]{0:T(1024)S(1)} %get-tuple-element.102) | copy-start | bytes 12292
  305.1 30.7 %all-to-all-start.6 = ((bf16[8,32,1024]{2,1,0:T(8,128)(2,1)}), bf16[8,32,1024]{2,1,0:T(8,128)(2,1)S(1)}, u32[]{:S(2)}, u32[]{:S(2)}) async-start(bf16[8,32,1024]{2,1,0:T(8,128)(2,1)} %broadcast_in_dim.21), calls=%async_computation.6 | async-start | bytes 1048576 | tf_op jit(solution)/shard_map/all_to_all | solution.py:24
  309.3 32.4 %copy-start.5 = (f32[40,1024]{1,0:T(8,128)S(1)}, f32[40,1024]{1,0:T(8,128)}, u32[]{:S(2)}) copy-start(f32[40,1024]{1,0:T(8,128)} %param.17) | copy-start | bytes 491524
  336.7 37.9 %all-to-all-start.4 = ((bf16[8,32,1280]{2,1,0:T(8,128)(2,1)}), bf16[8,32,1280]{2,1,0:T(8,128)(2,1)S(1)}, u32[]{:S(2)}, u32[]{:S(2)}) async-start(bf16[8,32,1280]{2,1,0:T(8,128)(2,1)} %broadcast_in_dim.9), calls=%async_computation.4 | async-start | bytes 1310720 | tf_op jit(solution)/shard_map/all_to_all | solution.py:24
  375.5 37.8 %all-to-all-start.5 = ((bf16[8,40,1024]{2,1,0:T(8,128)(2,1)}), bf16[8,40,1024]{2,1,0:T(8,128)(2,1)S(1)}, u32[]{:S(2)}, u32[]{:S(2)}) async-start(bf16[8,40,1024]{2,1,0:T(8,128)(2,1)} %broadcast_in_dim.20), calls=%async_computation.5 | async-start | bytes 1310720 | tf_op jit(solution)/shard_map/all_to_all | solution.py:24
where the time goes:
time: 417 us; the launch traced here: 416 us
  waiting for transfers between devices  172 us (41%)
  blocking collectives  169 us (41%)
  starting transfers between devices  33.2 us (8%)
  other arithmetic  19.8 us (5%)
  local copies, waits for them, and re-layouts  16.1 us (4%)
  between operations  5 us (1%)
    psum x9, blocking collectives, one_axis_at_a_time(): shard = lax.psum(shard, axis)  160 us
    all_to_all x3, waiting for transfers between devices, from_everyone(): return lax.all_to_all(copies, axis, split_axis=0, concat_axis=0, tiled=True)  91.1 us
    all_to_all x3, waiting for transfers between devices, reduce_gradient(): lax.all_to_all(gradient, 'dp', split_axis=1, concat_axis=0, tiled=True)  81.3 us
    all_to_all x3, starting transfers between devices, reduce_gradient(): lax.all_to_all(gradient, 'dp', split_axis=1, concat_axis=0, tiled=True)  21.1 us
    unnamed x51, local copies, waits for them, and re-layouts  13 us
    unnamed x3, other arithmetic  12.8 us
    all_to_all x3, starting transfers between devices, from_everyone(): return lax.all_to_all(copies, axis, split_axis=0, concat_axis=0, tiled=True)  12.1 us
    all_to_all x1, blocking collectives, from_everyone(): return lax.all_to_all(copies, axis, split_axis=0, concat_axis=0, tiled=True)  9.54 us
  transfers between devices with their start and end apart: 6, of which 6 were waited for; matrix products, arithmetic and copies ran while one was open for 4% of the time, Pallas kernels for 0%

commit v1 on v0

--- a/solution.py
+++ b/solution.py
@@ -43,7 +43,7 @@
 
 def one_axis_at_a_time(shard, axes):
     for axis in axes:
-        shard = lax.psum(shard, axis)
+        shard = jnp.sum(lax.all_gather(shard, axis), axis=0)
     return shard
 
 

time: 417 us -> 622 us (1.49)
  blocking collectives: 169 us -> 342 us
  local copies, waits for them, and re-layouts: 16.1 us -> 60.3 us
  waiting for transfers between devices: 172 us -> 139 us
  other arithmetic: 19.8 us -> 36.2 us
    all_gather x0 -> x12, blocking collectives: none -> 224 us  [one_axis_at_a_time(): shard = jnp.sum(lax.all_gather(shard, axis), axis=0)]
    psum x9 -> x0, blocking collectives: 160 us -> none  [one_axis_at_a_time(): shard = lax.psum(shard, axis)]
    unnamed x0 -> x9, blocking collectives: none -> 117 us
    unnamed x51 -> x110, local copies, waits for them, and re-layouts: 13 us -> 56.6 us
    all_to_all x3, waiting for transfers between devices: 81.3 us -> 49.4 us  [reduce_gradient(): lax.all_to_all(gradient, 'dp', split_axis=1, concat_axis=0, tiled=True)]
    reduce_sum x0 -> x39, other arithmetic: none -> 16.5 us  [one_axis_at_a_time(): shard = jnp.sum(lax.all_gather(shard, axis), axis=0)]
    all_to_all x1 -> x0, blocking collectives: 9.54 us -> none  [from_everyone(): return lax.all_to_all(copies, axis, split_axis=0, concat_axis=0, tiled=True)]
    all_to_all x3 -> x4, starting transfers between devices: 12.1 us -> 16.5 us  [from_everyone(): return lax.all_to_all(copies, axis, split_axis=0, concat_axis=0, tiled=True)]
  transfers between devices with their start and end apart: 6 -> 7, of which waited for: 6 -> 5; matrix products, arithmetic and copies ran while one was open for 4% -> 4% of each run, Pallas kernels for 0% -> 0%
where the time goes in v1:
time: 622 us; the launch traced here: 620 us
  blocking collectives  342 us (55%)
  waiting for transfers between devices  139 us (22%)
  local copies, waits for them, and re-layouts  60.3 us (10%)
  starting transfers between devices  37.6 us (6%)
  other arithmetic  36.2 us (6%)
    all_gather x12, blocking collectives, one_axis_at_a_time(): shard = jnp.sum(lax.all_gather(shard, axis), axis=0)  224 us
    unnamed x9, blocking collectives  117 us
    all_to_all x4, waiting for transfers between devices, from_everyone(): return lax.all_to_all(copies, axis, split_axis=0, concat_axis=0, tiled=True)  89.9 us
    unnamed x110, local copies, waits for them, and re-layouts  56.6 us
    all_to_all x3, waiting for transfers between devices, reduce_gradient(): lax.all_to_all(gradient, 'dp', split_axis=1, concat_axis=0, tiled=True)  49.4 us
    all_to_all x3, starting transfers between devices, reduce_gradient(): lax.all_to_all(gradient, 'dp', split_axis=1, concat_axis=0, tiled=True)  21.1 us
    all_to_all x4, starting transfers between devices, from_everyone(): return lax.all_to_all(copies, axis, split_axis=0, concat_axis=0, tiled=True)  16.5 us
    reduce_sum x39, other arithmetic, one_axis_at_a_time(): shard = jnp.sum(lax.all_gather(shard, axis), axis=0)  16.5 us
  transfers between devices with their start and end apart: 7, of which 5 were waited for; matrix products, arithmetic and copies ran while one was open for 4% of the time, Pallas kernels for 0%

profile of v1, /device:TPU:2, one launch (start us, length us, event | category | flops | bytes accessed | tf_op | source)
XLA Modules:
  0.0 620.4 jit_solution(1741721965191888897)
XLA Ops:
  0.6 1.9 copy.54
  3.0 3.7 reduce.33
  7.9 12.5 %all-to-all-start.2 = ((bf16[8,2,16384]{2,1,0:T(2,128)(2,1)}), bf16[8,2,16384]{2,1,0:T(2,128)(2,1)S(1)}, u32[]{:S(2)}, u32[]{:S(2)}) async-start(bf16[8,2,16384]{2,1,0:T(2,128)(2,1)} %reshape.231), calls=%async_computation.2 | async-start | bytes 1048576 | tf_op jit(solution)/shard_map/all_to_all | solution.py:59
  21.4 4.6 reduce.32
  27.1 22.1 %all-to-all-done.2 = bf16[8,2,16384]{2,1,0:T(2,128)(2,1)S(1)} async-done(((bf16[8,2,16384]{2,1,0:T(2,128)(2,1)}), bf16[8,2,16384]{2,1,0:T(2,128)(2,1)S(1)}, u32[]{:S(2)}, u32[]{:S(2)}) %all-to-all-start.2) | async-done | bytes 524320 | tf_op jit(solution)/shard_map/all_to_all | solution.py:59
  49.2 4.3 all-to-all-start
  54.4 4.5 reduce.34
  60.2 27.3 %all-to-all-done = bf16[8,2,20480]{2,1,0:T(2,128)(2,1)S(1)} async-done(((bf16[8,2,20480]{2,1,0:T(2,128)(2,1)}), bf16[8,2,20480]{2,1,0:T(2,128)(2,1)S(1)}, u32[]{:S(2)}, u32[]{:S(2)}) %all-to-all-start) | async-done | bytes 655392 | tf_op jit(solution)/shard_map/all_to_all | solution.py:59
  87.4 4.3 all-to-all-start.1
  97.7 50.9 %all-gather.8 = f32[8192]{0:T(1024)S(1)} all-gather(f32[1024]{0:T(1024)S(1)} %get-tuple-element.19), channel_id=10, replica_groups=mesh['dp'=8,'row_0'=2,'row_1'=4,'row_2'=2,'col'=4] {'dp'}, dimensions={0}, use_global_device_ids=true | all-gather | bytes 36864 | tf_op jit(solution)/shard_map/all_gather | solution.py:46
  148.7 13.1 %all-gather.9 = f32[2048]{0:T(1024)S(1)} all-gather(f32[1024]{0:T(1024)S(1)} %reduce_sum.540), channel_id=11, replica_groups=mesh['dp'=8,'row_0'=2,'row_1'=4,'row_2'=2,'col'=4] {'row_0'}, dimensions={0}, use_global_device_ids=true | all-gather | bytes 12288 | tf_op jit(solution)/shard_map/all_gather | solution.py:46
  161.8 12.1 %all-gather.10 = f32[4096]{0:T(1024)S(1)} all-gather(f32[1024]{0:T(1024)S(1)} %reduce_sum.541), channel_id=12, replica_groups=mesh['dp'=8,'row_0'=2,'row_1'=4,'row_2'=2,'col'=4] {'row_1'}, dimensions={0}, use_global_device_ids=true | all-gather | bytes 20480 | tf_op jit(solution)/shard_map/all_gather | solution.py:46
  173.9 1.8 all-gather.11
  176.7 46.4 %all-gather.12 = f32[8,1,1280]{2,1,0:T(1,128)S(1)} all-gather(f32[1,1,1280]{2,1,0:T(1,128)S(1)} %reshape.163), channel_id=2, replica_groups=mesh['dp'=8,'row_0'=2,'row_1'=4,'row_2'=2,'col'=4] {'dp'}, dimensions={0}, use_global_device_ids=true | all-gather | bytes 46080 | tf_op jit(solution)/shard_map/all_gather | solution.py:46
  223.1 13.1 %all-gather.13 = f32[2,1,1280]{2,1,0:T(1,128)S(1)} all-gather(f32[1,1,1280]{2,1,0:T(1,128)S(1)} %reshape.165), channel_id=3, replica_groups=mesh['dp'=8,'row_0'=2,'row_1'=4,'row_2'=2,'col'=4] {'row_0'}, dimensions={0}, use_global_device_ids=true | all-gather | bytes 15360 | tf_op jit(solution)/shard_map/all_gather | solution.py:46
  236.3 12.0 %all-gather.14 = f32[4,1,1280]{2,1,0:T(1,128)S(1)} all-gather(f32[1,1,1280]{2,1,0:T(1,128)S(1)} %reshape.167), channel_id=4, replica_groups=mesh['dp'=8,'row_0'=2,'row_1'=4,'row_2'=2,'col'=4] {'row_1'}, dimensions={0}, use_global_device_ids=true | all-gather | bytes 25600 | tf_op jit(solution)/shard_map/all_gather | solution.py:46
  248.3 1.8 all-gather.15
  252.0 4.5 all-to-all-start.3
  256.5 46.3 %all-gather.4 = f32[8192]{0:T(1024)S(1)} all-gather(f32[1024]{0:T(1024)S(1)} %get-tuple-element.15), channel_id=6, replica_groups=mesh['dp'=8,'row_0'=2,'row_1'=4,'row_2'=2,'col'=4] {'dp'}, dimensions={0}, use_global_device_ids=true | all-gather | bytes 36864 | tf_op jit(solution)/shard_map/all_gather | solution.py:46
  302.8 13.1 %all-gather.5 = f32[2048]{0:T(1024)S(1)} all-gather(f32[1024]{0:T(1024)S(1)} %reduce_sum.524), channel_id=7, replica_groups=mesh['dp'=8,'row_0'=2,'row_1'=4,'row_2'=2,'col'=4] {'row_0'}, dimensions={0}, use_global_device_ids=true | all-gather | bytes 12288 | tf_op jit(solution)/shard_map/all_gather | solution.py:46
  315.9 12.0 %all-gather.6 = f32[4096]{0:T(1024)S(1)} all-gather(f32[1024]{0:T(1024)S(1)} %reduce_sum.525), channel_id=8, replica_groups=mesh['dp'=8,'row_0'=2,'row_1'=4,'row_2'=2,'col'=4] {'row_1'}, dimensions={0}, use_global_device_ids=true | all-gather | bytes 20480 | tf_op jit(solution)/shard_map/all_gather | solution.py:46
  329.4 1.4 dynamic-update-slice
  330.8 1.4 dynamic-update-slice.9
  332.2 1.4 dynamic-update-slice.18
  333.6 1.8 all-gather.7
  335.4 30.6 %all-reduce.28 = (f32[8]{0:T(128)S(1)}, f32[8]{0:T(128)S(1)}, f32[8]{0:T(128)S(1)}) all-reduce(f32[8]{0:T(128)S(1)} %dynamic-update-slice, f32[8]{0:T(128)S(1)} %dynamic-update-slice.9, f32[8]{0:T(128)S(1)} %dynamic-update-slice.18), channel_id=1, replica_groups=mesh['dp'=8,'row_0'=2,'row_1'=4,'row_2'=2,'col'=4] {'dp'}, use_global_device_ids=true, to_apply=%add | all-reduce | flops 24 | bytes 192
  367.3 1.4 dynamic-update-slice.1
  368.7 1.4 dynamic-update-slice.10
  370.7 1.4 dynamic-update-slice.19
  372.1 13.6 %all-reduce.35 = (f32[2]{0:T(128)S(1)}, f32[2]{0:T(128)S(1)}, f32[2]{0:T(128)S(1)}) all-reduce(f32[2]{0:T(128)S(1)} %dynamic-update-slice.1, f32[2]{0:T(128)S(1)} %dynamic-update-slice.10, f32[2]{0:T(128)S(1)} %dynamic-update-slice.19), channel_id=1, replica_groups=mesh['dp'=8,'row_0'=2,'row_1'=4,'row_2'=2,'col'=4] {'row_0'}, use_global_device_ids=true, to_apply=%add.1 | all-reduce | flops 6 | bytes 48
  386.9 1.4 dynamic-update-slice.2
  388.3 1.4 dynamic-update-slice.11
  390.3 1.4 dynamic-update-slice.20
  391.8 8.6 %all-reduce.31 = (f32[4]{0:T(128)S(1)}, f32[4]{0:T(128)S(1)}, f32[4]{0:T(128)S(1)}) all-reduce(f32[4]{0:T(128)S(1)} %dynamic-update-slice.2, f32[4]{0:T(128)S(1)} %dynamic-update-slice.11, f32[4]{0:T(128)S(1)} %dynamic-update-slice.20), channel_id=1, replica_groups=mesh['dp'=8,'row_0'=2,'row_1'=4,'row_2'=2,'col'=4] {'row_1'}, use_global_device_ids=true, to_apply=%add.2 | all-reduce | flops 12 | bytes 96
  401.5 1.4 dynamic-update-slice.3
  402.9 1.4 dynamic-update-slice.12
  404.9 1.4 dynamic-update-slice.21
  406.4 2.5 all-reduce.33
  412.1 1.5 dynamic-update-slice.4
  415.7 1.4 dynamic-update-slice.13
  417.8 1.4 dynamic-update-slice.22
  419.2 25.0 %all-reduce.27 = (f32[8]{0:T(128)S(1)}, f32[8]{0:T(128)S(1)}, f32[8]{0:T(128)S(1)}) all-reduce(f32[8]{0:T(128)S(1)} %dynamic-update-slice.4, f32[8]{0:T(128)S(1)} %dynamic-update-slice.13, f32[8]{0:T(128)S(1)} %dynamic-update-slice.22), channel_id=1, replica_groups=mesh['dp'=8,'row_0'=2,'row_1'=4,'row_2'=2,'col'=4] {'dp'}, use_global_device_ids=true, to_apply=%add.4 | all-reduce | flops 24 | bytes 192
  444.9 1.4 dynamic-update-slice.5
  446.9 1.4 dynamic-update-slice.14
  448.9 1.4 dynamic-update-slice.23
  450.3 13.6 %all-reduce.34 = (f32[2]{0:T(128)S(1)}, f32[2]{0:T(128)S(1)}, f32[2]{0:T(128)S(1)}) all-reduce(f32[2]{0:T(128)S(1)} %dynamic-update-slice.5, f32[2]{0:T(128)S(1)} %dynamic-update-slice.14, f32[2]{0:T(128)S(1)} %dynamic-update-slice.23), channel_id=1, replica_groups=mesh['dp'=8,'row_0'=2,'row_1'=4,'row_2'=2,'col'=4] {'row_0'}, use_global_device_ids=true, to_apply=%add.5 | all-reduce | flops 6 | bytes 48
  464.5 1.4 dynamic-update-slice.6
  466.5 1.4 dynamic-update-slice.15
  468.5 1.4 dynamic-update-slice.24
  469.9 10.1 %all-reduce.30 = (f32[4]{0:T(128)S(1)}, f32[4]{0:T(128)S(1)}, f32[4]{0:T(128)S(1)}) all-reduce(f32[4]{0:T(128)S(1)} %dynamic-update-slice.6, f32[4]{0:T(128)S(1)} %dynamic-update-slice.15, f32[4]{0:T(128)S(1)} %dynamic-update-slice.24), channel_id=1, replica_groups=mesh['dp'=8,'row_0'=2,'row_1'=4,'row_2'=2,'col'=4] {'row_1'}, use_global_device_ids=true, to_apply=%add.6 | all-reduce | flops 12 | bytes 96
  480.6 1.4 dynamic-update-slice.7
  482.6 1.4 dynamic-update-slice.16
  484.6 1.4 dynamic-update-slice.25
  487.3 2.4 all-reduce.32
  490.9 1.4 dynamic-update-slice.8
  492.3 1.4 dynamic-update-slice.17
  494.3 1.4 dynamic-update-slice.26
  495.7 10.9 %all-reduce.29 = (f32[4]{0:T(128)S(1)}, f32[4]{0:T(128)S(1)}, f32[4]{0:T(128)S(1)}) all-reduce(f32[4]{0:T(128)S(1)} %dynamic-update-slice.8, f32[4]{0:T(128)S(1)} %dynamic-update-slice.17, f32[4]{0:T(128)S(1)} %dynamic-update-slice.26), channel_id=1, replica_groups=mesh['dp'=8,'row_0'=2,'row_1'=4,'row_2'=2,'col'=4] {'col'}, use_global_device_ids=true, to_apply=%add.8 | all-reduce | flops 12 | bytes 96
  509.7 3.5 all-to-all-start.6
  515.4 25.0 %all-to-all-done.6 = bf16[8,32,1024]{2,1,0:T(8,128)(2,1)S(1)} async-done(((bf16[8,32,1024]{2,1,0:T(8,128)(2,1)}), bf16[8,32,1024]{2,1,0:T(8,128)(2,1)S(1)}, u32[]{:S(2)}, u32[]{:S(2)}) %all-to-all-start.6) | async-done | bytes 524320 | tf_op jit(solution)/shard_map/all_to_all | solution.py:24
  541.3 4.3 all-to-all-start.4
  547.8 31.4 %all-to-all-done.4 = bf16[8,32,1280]{2,1,0:T(8,128)(2,1)S(1)} async-done(((bf16[8,32,1280]{2,1,0:T(8,128)(2,1)}), bf16[8,32,1280]{2,1,0:T(8,128)(2,1)S(1)}, u32[]{:S(2)}, u32[]{:S(2)}) %all-to-all-start.4) | async-done | bytes 655392 | tf_op jit(solution)/shard_map/all_to_all | solution.py:24
  580.1 4.3 all-to-all-start.5
  584.4 33.5 %all-to-all-done.5 = bf16[8,40,1024]{2,1,0:T(8,128)(2,1)S(1)} async-done(((bf16[8,40,1024]{2,1,0:T(8,128)(2,1)}), bf16[8,40,1024]{2,1,0:T(8,128)(2,1)S(1)}, u32[]{:S(2)}, u32[]{:S(2)}) %all-to-all-start.5) | async-done | bytes 655392 | tf_op jit(solution)/shard_map/all_to_all | solution.py:24
  (157 shorter events, 44.0 us)
Async XLA Ops:
  6.7 13.7 %copy-start = (bf16[1,256,1280]{2,1,0:T(8,128)(2,1)S(1)}, bf16[1,256,1280]{2,1,0:T(8,128)(2,1)}, u32[]{:S(2)}) copy-start(bf16[1,256,1280]{2,1,0:T(8,128)(2,1)} %param.12) | copy-start | bytes 1966084
  7.9 41.3 %all-to-all-start.2 = ((bf16[8,2,16384]{2,1,0:T(2,128)(2,1)}), bf16[8,2,16384]{2,1,0:T(2,128)(2,1)S(1)}, u32[]{:S(2)}, u32[]{:S(2)}) async-start(bf16[8,2,16384]{2,1,0:T(2,128)(2,1)} %reshape.231), calls=%async_computation.2 | async-start | bytes 1048576 | tf_op jit(solution)/shard_map/all_to_all | solution.py:59
  27.1 26.4 %copy-start.1 = (bf16[1,320,1024]{2,1,0:T(8,128)(2,1)S(1)}, bf16[1,320,1024]{2,1,0:T(8,128)(2,1)}, u32[]{:S(2)}) copy-start(bf16[1,320,1024]{2,1,0:T(8,128)(2,1)} %param.16) | copy-start | bytes 1966084
  49.2 38.3 %all-to-all-start = ((bf16[8,2,20480]{2,1,0:T(2,128)(2,1)}), bf16[8,2,20480]{2,1,0:T(2,128)(2,1)S(1)}, u32[]{:S(2)}, u32[]{:S(2)}) async-start(bf16[8,2,20480]{2,1,0:T(2,128)(2,1)} %reshape.229), calls=%async_computation | async-start | bytes 1310720 | tf_op jit(solution)/shard_map/all_to_all | solution.py:59
  87.4 162.7 %all-to-all-start.1 = ((bf16[8,2,20480]{2,1,0:T(2,128)(2,1)}), bf16[8,2,20480]{2,1,0:T(2,128)(2,1)S(1)}, u32[]{:S(2)}, u32[]{:S(2)}) async-start(bf16[8,2,20480]{2,1,0:T(2,128)(2,1)} %reshape.233), calls=%async_computation.1 | async-start | bytes 1310720 | tf_op jit(solution)/shard_map/all_to_all | solution.py:59
  97.3 78.4 %copy-start.12 = (f32[1024]{0:T(1024)S(1)}, f32[1024]{0:T(1024)}, u32[]{:S(2)}) copy-start(f32[1024]{0:T(1024)} %param.23) | copy-start | bytes 12292
  175.7 332.2 %copy-start.6 = (f32[1024]{0:T(1024)}, f32[1024]{0:T(1024)S(1)}, u32[]{:S(2)}) copy-start(f32[1024]{0:T(1024)S(1)} %multiply_add_fusion.4) | copy-start | bytes 12292
  250.8 65.1 %copy-start.8 = (f32[1280]{0:T(1024)S(1)}, f32[1280]{0:T(1024)}, u32[]{:S(2)}) copy-start(f32[1280]{0:T(1024)} %param.15) | copy-start | bytes 15364
  250.8 77.2 %copy-start.14 = (f32[40]{0:T(128)S(1)}, f32[40]{0:T(128)}, u32[]{:S(2)}) copy-start(f32[40]{0:T(128)} %param.18) | copy-start | bytes 484
  250.8 77.9 %copy-start.15 = (f32[32]{0:T(128)S(1)}, f32[32]{0:T(128)}, u32[]{:S(2)}) copy-start(f32[32]{0:T(128)} %param.22) | copy-start | bytes 388
  250.9 77.8 %copy-start.16 = (f32[32]{0:T(128)S(1)}, f32[32]{0:T(128)}, u32[]{:S(2)}) copy-start(f32[32]{0:T(128)} %param.14) | copy-start | bytes 388
  250.9 155.5 %copy-start.13 = (f32[1024]{0:T(1024)S(1)}, f32[1024]{0:T(1024)}, u32[]{:S(2)}) copy-start(f32[1024]{0:T(1024)} %param.19) | copy-start | bytes 12292
  251.1 256.9 %copy-start.4 = (f32[32,1024]{1,0:T(8,128)S(1)}, f32[32,1024]{1,0:T(8,128)}, u32[]{:S(2)}) copy-start(f32[32,1024]{1,0:T(8,128)} %param.21) | copy-start | bytes 393220
  252.0 76.0 %all-to-all-start.3 = ((f32[4,1,104]{2,1,0:T(1,128)}), f32[4,1,104]{2,1,0:T(1,128)S(1)}, u32[]{:S(2)}, u32[]{:S(2)}) async-start(f32[4,1,104]{2,1,0:T(1,128)} %broadcast_in_dim.8), calls=%async_computation.3 | async-start | bytes 4096 | tf_op jit(solution)/shard_map/all_to_all | solution.py:24
  315.9 198.6 %copy-start.5 = (f32[1280]{0:T(1024)}, f32[1280]{0:T(1024)S(1)}, u32[]{:S(2)}) copy-start(f32[1280]{0:T(1024)S(1)} %multiply_add_fusion.3) | copy-start | bytes 15364
  328.7 218.2 %copy-start.9 = (f32[40]{0:T(128)}, f32[40]{0:T(128)S(1)}, u32[]{:S(2)}) copy-start(f32[40]{0:T(128)S(1)} %get-tuple-element.87) | copy-start | bytes 484
  329.4 180.3 %copy-start.11 = (f32[32]{0:T(128)}, f32[32]{0:T(128)S(1)}, u32[]{:S(2)}) copy-start(f32[32]{0:T(128)S(1)} %get-tuple-element.92) | copy-start | bytes 388
  329.4 185.1 %copy-start.10 = (f32[32]{0:T(128)}, f32[32]{0:T(128)S(1)}, u32[]{:S(2)}) copy-start(f32[32]{0:T(128)S(1)} %get-tuple-element.82) | copy-start | bytes 388
  406.4 140.6 %copy-start.7 = (f32[1024]{0:T(1024)}, f32[1024]{0:T(1024)S(1)}, u32[]{:S(2)}) copy-start(f32[1024]{0:T(1024)S(1)} %multiply_add_fusion.5) | copy-start | bytes 12292
  414.9 99.6 %copy-start.2 = (f32[32,1280]{1,0:T(8,128)S(1)}, f32[32,1280]{1,0:T(8,128)}, u32[]{:S(2)}) copy-start(f32[32,1280]{1,0:T(8,128)} %param.13) | copy-start | bytes 491524
  509.7 30.7 %all-to-all-start.6 = ((bf16[8,32,1024]{2,1,0:T(8,128)(2,1)}), bf16[8,32,1024]{2,1,0:T(8,128)(2,1)S(1)}, u32[]{:S(2)}, u32[]{:S(2)}) async-start(bf16[8,32,1024]{2,1,0:T(8,128)(2,1)} %broadcast_in_dim.21), calls=%async_computation.6 | async-start | bytes 1048576 | tf_op jit(solution)/shard_map/all_to_all | solution.py:24
  514.5 32.4 %copy-start.3 = (f32[40,1024]{1,0:T(8,128)S(1)}, f32[40,1024]{1,0:T(8,128)}, u32[]{:S(2)}) copy-start(f32[40,1024]{1,0:T(8,128)} %param.17) | copy-start | bytes 491524
  541.3 37.9 %all-to-all-start.4 = ((bf16[8,32,1280]{2,1,0:T(8,128)(2,1)}), bf16[8,32,1280]{2,1,0:T(8,128)(2,1)S(1)}, u32[]{:S(2)}, u32[]{:S(2)}) async-start(bf16[8,32,1280]{2,1,0:T(8,128)(2,1)} %broadcast_in_dim.9), calls=%async_computation.4 | async-start | bytes 1310720 | tf_op jit(solution)/shard_map/all_to_all | solution.py:24
  580.1 37.8 %all-to-all-start.5 = ((bf16[8,40,1024]{2,1,0:T(8,128)(2,1)}), bf16[8,40,1024]{2,1,0:T(8,128)(2,1)S(1)}, u32[]{:S(2)}, u32[]{:S(2)}) async-start(bf16[8,40,1024]{2,1,0:T(8,128)(2,1)} %broadcast_in_dim.20), calls=%async_computation.5 | async-start | bytes 1310720 | tf_op jit(solution)/shard_map/all_to_all | solution.py:24
